TPU v7x, 32 devices: a whole 2x2x4 slice. The times are simulated.
32 devices in a mesh: samp: 8 (over y, x, core), cpg: 4 (over z).
Axes of the slice: x: 2, y: 2, z: 4, core: 2. Of those that a mesh axis runs over, the one named last changes fastest.
Arguments:
- responses: bfloat16 [256, 16384], P('samp', 'cpg'), may hold values from -5 to 5
- weights: bfloat16 [256, 16384], P('samp', 'cpg'), may hold values from 1 to 8
- phenotype: float32 [16384], P('cpg'), may hold values from -6 to 6
- eigvecs: bfloat16 [16384, 16384], P('cpg', 'samp'), may hold values from -0.046875 to 0.046875
- eigvals: float32 [16384], P('samp'), may hold values from 0.0001 to 1
- positions: int32 [256], replicated, may hold values from 1 to 76800, as said below
- reaches: int32 [256], P('cpg'), may hold values from 1 to 8
Outputs:
- smoothed: float32 [256], P('cpg')
- log_scale: float32 [256], P('cpg')
Inputs may be any that keep to these rules, and one draw needn't show every extreme that they name: CpG m (from 0) lies at 300 m plus an offset of 1 to 300, so positions strictly increase and consecutive CpGs lie 1 to 599 base pairs apart.
All inputs are finite; a program needn't handle non-finite values.
Results may differ from a plain program's by a relative error of at most 0.0041.
Values may be sent and summed in bfloat16 or wider, within the bound.
A program may use at most 64 MiB of HBM per device.

v0:
```python
import jax
import jax.numpy as jnp
from jax import lax
from jax.sharding import PartitionSpec as P

ITERS = 4
HALO = 8
EPSILON = 1e-06
band_width = 1000.0


def padded(value, sides, width):
    for axis, dim in sides:
        peers, length = (lax.axis_size(axis), value.shape[dim])
        up = [(i, (i + 1) % peers) for i in range(peers - 1)]
        down = [(j, i) for i, j in up]
        last = lax.slice_in_dim(value, length - width, length, axis=dim)
        leading = lax.slice_in_dim(value, 0, width, axis=dim)
        before = lax.ppermute(last, axis, up)
        after = lax.ppermute(leading, axis, down)
        value = jnp.concatenate([before, value, after], axis=dim)
    return value


def smooth_block(widened, places, present, reaches):
    block_len = reaches.shape[0]
    centre = places[HALO : HALO + block_len]
    total_sum = jnp.zeros((block_len,), jnp.float32)
    norm_sum = jnp.zeros((block_len,), jnp.float32)
    for offset in range(2 * HALO + 1):
        near_scores = widened[offset : offset + block_len]
        near_places = places[offset : offset + block_len]
        within = (abs(offset - HALO) <= reaches).astype(jnp.float32)
        kernel = (
            present[offset : offset + block_len]
            * within
            * jnp.exp(-jnp.abs(near_places - centre) / band_width)
        )
        total_sum = total_sum + kernel * near_scores
        norm_sum = norm_sum + kernel
    return total_sum / norm_sum


def fit_scores(rot_resp, rot_design, eigen_part, sum_axis, fit_total, score_total):
    log_scale = jnp.zeros((rot_resp.shape[1 - sum_axis],), jnp.float32)
    for repeat in range(ITERS):
        inverse = 1.0 / (jnp.expand_dims(jnp.exp(log_scale), sum_axis) * eigen_part + 1.0)
        design_over = rot_design * inverse
        crossed_part = jnp.sum(design_over * rot_resp, axis=sum_axis)
        energy_part = jnp.sum(design_over * rot_design, axis=sum_axis)
        leverage = eigen_part * inverse
        traced_part = jnp.sum(leverage + 0.0 * inverse, axis=sum_axis)
        fisher_part = jnp.sum(leverage * leverage, axis=sum_axis)
        scaled = leverage * inverse
        resp_part = jnp.sum(scaled * rot_resp * rot_resp, axis=sum_axis)
        mixed_part = jnp.sum(scaled * rot_design * rot_resp, axis=sum_axis)
        design_part = jnp.sum(scaled * rot_design * rot_design, axis=sum_axis)
        crossed, energy, traced, fisher, resp_spread, mixed_spread, design_spread = fit_total(
            (
                crossed_part,
                energy_part,
                traced_part,
                fisher_part,
                resp_part,
                mixed_part,
                design_part,
            )
        )
        energy = energy + EPSILON
        effect = crossed / energy
        spread = resp_spread - 2.0 * effect * mixed_spread + effect * effect * design_spread
        gradient = 0.5 * (spread - traced)
        log_scale = log_scale + jnp.tanh(gradient / (jnp.exp(log_scale) * (0.5 * fisher)))
    inverse = 1.0 / (jnp.expand_dims(jnp.exp(log_scale), sum_axis) * eigen_part + 1.0)
    design_over = rot_design * inverse
    crossed, energy = score_total(
        (
            jnp.sum(design_over * rot_resp, axis=sum_axis),
            jnp.sum(design_over * rot_design, axis=sum_axis),
        )
    )
    return (crossed / jnp.sqrt(energy + EPSILON), log_scale)


def shards(responses, weights, phenotype, eigvecs, eigvals, positions, reaches):
    root_weight = jnp.sqrt(weights.astype(jnp.float32))
    weighted = (root_weight * responses.astype(jnp.float32)).astype(jnp.bfloat16)
    design = (root_weight * phenotype[None, :]).astype(jnp.bfloat16)
    all_resp, all_design = (
        lax.all_gather(weighted, "samp", axis=0, tiled=True),
        lax.all_gather(design, "samp", axis=0, tiled=True),
    )
    cpg_count = lax.axis_size("cpg")
    block_len = reaches.shape[0]
    total_cpgs = block_len * cpg_count
    base = lax.axis_index("cpg") * block_len

    def fit_block(partials):
        return lax.psum(partials, "samp")

    def score_block(partials):
        return lax.psum(partials, "samp")

    rotated = lax.psum_scatter(
        jnp.concatenate(
            [
                jnp.dot(all_resp, eigvecs, preferred_element_type=jnp.float32),
                jnp.dot(all_design, eigvecs, preferred_element_type=jnp.float32),
            ],
            axis=1,
        ),
        "cpg",
        scatter_dimension=0,
        tiled=True,
    )
    comp_width = eigvecs.shape[1]
    scores, log_scale = fit_scores(
        rotated[:, :comp_width],
        rotated[:, comp_width:],
        eigvals[None, :],
        1,
        fit_block,
        score_block,
    )
    widened = padded(scores, (("cpg", 0),), HALO)
    places = lax.dynamic_slice_in_dim(
        jnp.pad(positions.astype(jnp.float32), HALO), base, block_len + 2 * HALO, 0
    )
    global_index = base - HALO + jnp.arange(block_len + 2 * HALO, dtype=jnp.int32)
    present = ((global_index >= 0) & (global_index < total_cpgs)).astype(jnp.float32)
    smoothed = smooth_block(widened, places, present, reaches)
    return (smoothed, log_scale)


def solution(mesh):
    in_specs = (
        P("samp", "cpg"),
        P("samp", "cpg"),
        P("cpg"),
        P("cpg", "samp"),
        P("samp"),
        P(),
        P("cpg"),
    )
    out_specs = (P("cpg"), P("cpg"))
    return jax.shard_map(shards, mesh=mesh, in_specs=in_specs, out_specs=out_specs, check_vma=False)
```

profile of v0, /device:TPU:0, one launch (start us, length us, event | category | flops | bytes accessed | tf_op | source)
XLA Modules:
  0.0 242.1 jit_solution(15517261634825529933)
XLA Ops:
  7.2 0.0 all-gather.3.cloned.1.call-start
  7.2 2.0 multiply_convert_fusion.1
  9.3 0.0 all-gather.3.cloned.1.call-update
  9.3 0.0 all-gather.5.cloned.1.call-start
  9.3 0.7 all-gather.5.cloned.1.call-update
  10.0 0.0 reduce-scatter.2.cloned.1.call-start
  10.1 30.3 %all-gather.3.cloned.1.call-done = bf16[256,4096]{1,0:T(8,128)(2,1)} async-done(((bf16[32,4096]{1,0:T(8,128)(2,1)}), bf16[256,4096]{1,0:T(8,128)(2,1)}) %all-gather.3.cloned.1.call-update) | async-done | bytes 2097168 | tf_op jit(solution)/shard_map/all_gather | solution.py:90
  40.4 8.7 %fusion.38 = f32[256,2048]{1,0:T(8,128)S(1)} fusion(bf16[256,4096]{1,0:T(8,128)(2,1)} %all-gather.3.cloned.1.call-done, bf16[4096,2048]{1,0:T(8,128)(2,1)} %param.10), kind=kOutput, calls=%fused_computation.110 | convolution fusion | flops 4294967296 | bytes 20971520 | tf_op jit(solution)/shard_map/dot_general | solution.py:107
  49.1 21.0 %all-gather.5.cloned.1.call-done = bf16[256,4096]{1,0:T(8,128)(2,1)} async-done(((bf16[32,4096]{1,0:T(8,128)(2,1)}), bf16[256,4096]{1,0:T(8,128)(2,1)}) %all-gather.5.cloned.1.call-update) | async-done | bytes 2097168 | tf_op jit(solution)/shard_map/all_gather | solution.py:91
  70.1 8.7 %fusion.39 = f32[256,2048]{1,0:T(8,128)S(1)} fusion(bf16[256,4096]{1,0:T(8,128)(2,1)} %all-gather.5.cloned.1.call-done, bf16[4096,2048]{1,0:T(8,128)(2,1)} %param.10), kind=kOutput, calls=%fused_computation.111 | convolution fusion | flops 4294967296 | bytes 20971520 | tf_op jit(solution)/shard_map/dot_general | solution.py:108
  78.8 2.3 pad_maximum_fusion
  81.1 0.0 copy-start.2
  81.1 0.0 copy-start.1
  81.1 0.0 reduce-scatter.2.cloned.1.call-update
  81.2 0.6 copy-done.2
  81.8 0.1 pad_dynamic-slice_fusion
  81.9 0.0 copy-done.1
  81.9 0.6 multiply_multiply_fusion.14
  82.5 75.6 %reduce-scatter.2.cloned.1.call-done = f32[64,4096]{1,0:T(8,128)} async-done(((f32[256,4096]{1,0:T(8,128)}), f32[64,4096]{1,0:T(8,128)}) %reduce-scatter.2.cloned.1.call-update) | async-done | bytes 1048592 | tf_op jit(solution)/shard_map/reduce_scatter | solution.py:104
  158.1 0.0 copy-start
  158.1 1.7 fusion.7
  159.8 0.7 reduce_sum.280
  160.5 0.6 reduce_sum.282
  161.1 13.3 %all-reduce.5 = (f32[64]{0:T(128)S(1)}, f32[64]{0:T(128)S(1)}, f32[64]{0:T(128)S(1)}, f32[64]{0:T(128)S(1)}, f32[64]{0:T(128)S(1)}, /*index=5*/f32[64]{0:T(128)S(1)}, f32[64]{0:T(128)S(1)}) all-reduce(f32[64]{0:T(128)S(1)} %reduce_sum.282, f32[64]{0:T(128)S(1)} %reduce_sum.280, ...), channel_id=1, replica_groups=mesh['samp'=8,'cpg'=4] {'samp'}, use_global_device_ids=true, to_apply=%region_14.0 | all-reduce | flops 448 | bytes 3584 | tf_op jit(solution)/shard_map/psum | solution.py:99
  174.4 0.0 copy-start.3
  174.4 1.9 multiply_reduce_fusion.12
  176.3 11.8 %all-reduce.4 = (f32[64]{0:T(128)S(1)}, f32[64]{0:T(128)S(1)}, f32[64]{0:T(128)S(1)}, f32[64]{0:T(128)S(1)}, f32[64]{0:T(128)S(1)}, /*index=5*/f32[64]{0:T(128)S(1)}, f32[64]{0:T(128)S(1)}) all-reduce(f32[64]{0:T(128)S(1)} %get-tuple-element.31, f32[64]{0:T(128)S(1)} %get-tuple-element.32, ...), channel_id=1, replica_groups=mesh['samp'=8,'cpg'=4] {'samp'}, use_global_device_ids=true, to_apply=%region_28.0 | all-reduce | flops 448 | bytes 3584 | tf_op jit(solution)/shard_map/psum | solution.py:99
  188.2 0.0 copy-done
  188.2 0.6 multiply_reduce_fusion.8
  188.8 11.8 %all-reduce.3 = (f32[64]{0:T(128)S(1)}, f32[64]{0:T(128)S(1)}, f32[64]{0:T(128)S(1)}, f32[64]{0:T(128)S(1)}, f32[64]{0:T(128)S(1)}, /*index=5*/f32[64]{0:T(128)S(1)}, f32[64]{0:T(128)S(1)}) all-reduce(f32[64]{0:T(128)S(1)} %get-tuple-element.29, f32[64]{0:T(128)S(1)} %get-tuple-element.30, ...), channel_id=1, replica_groups=mesh['samp'=8,'cpg'=4] {'samp'}, use_global_device_ids=true, to_apply=%region_42.0 | all-reduce | flops 448 | bytes 3584 | tf_op jit(solution)/shard_map/psum | solution.py:99
  200.6 0.6 multiply_reduce_fusion.4
  201.2 11.8 %all-reduce.2 = (f32[64]{0:T(128)S(1)}, f32[64]{0:T(128)S(1)}, f32[64]{0:T(128)S(1)}, f32[64]{0:T(128)S(1)}, f32[64]{0:T(128)S(1)}, /*index=5*/f32[64]{0:T(128)S(1)}, f32[64]{0:T(128)S(1)}) all-reduce(f32[64]{0:T(128)S(1)} %get-tuple-element.27, f32[64]{0:T(128)S(1)} %get-tuple-element.28, ...), channel_id=1, replica_groups=mesh['samp'=8,'cpg'=4] {'samp'}, use_global_device_ids=true, to_apply=%region_56.0 | all-reduce | flops 448 | bytes 3584 | tf_op jit(solution)/shard_map/psum | solution.py:99
  213.0 0.5 fusion.32
  213.6 0.3 multiply_reduce_fusion
  213.9 11.8 %all-reduce.1 = (f32[64]{0:T(128)S(1)}, f32[64]{0:T(128)S(1)}) all-reduce(f32[64]{0:T(128)S(1)} %get-tuple-element.3, f32[64]{0:T(128)S(1)} %get-tuple-element.2), channel_id=1, replica_groups=mesh['samp'=8,'cpg'=4] {'samp'}, use_global_device_ids=true, to_apply=%region_58.0 | all-reduce | flops 128 | bytes 1024 | tf_op jit(solution)/shard_map/psum | solution.py:102
  225.7 0.1 fusion.37
  225.7 3.6 %collective-permute-start = (f32[8]{0:T(128)S(1)}, f32[8]{0:T(128)S(1)}, u32[]{:S(2)}, u32[]{:S(2)}) collective-permute-start(f32[8]{0:T(128)S(1)} %get-tuple-element.81), channel_id=1, source_target_pairs={{0,1},{1,2},{2,3},{4,5},{5,6},{6,7},{8,9},{9,10},{10,11},{12,13},{... | collective-permute-start | bytes 104 | tf_op jit(solution)/shard_map/ppermute | solution.py:19
  229.4 1.3 collective-permute-start.1
  230.7 0.0 collective-permute-done
  230.7 4.2 %collective-permute-done.1 = f32[8]{0:T(128)S(1)} collective-permute-done((f32[8]{0:T(128)S(1)}, f32[8]{0:T(128)S(1)}, u32[]{:S(2)}, u32[]{:S(2)}) %collective-permute-start.1) | collective-permute-done | bytes 64 | tf_op jit(solution)/shard_map/ppermute | solution.py:20
  234.9 0.1 pad_maximum_fusion.1
  235.0 0.0 copy-done.3
  235.0 0.6 add_divide_fusion.4
  (6 shorter events, 0.1 us)
Async XLA Ops:
  7.2 33.2 %all-gather.3.cloned.1.call-start = ((), (), s32[]{:S(2)}) async-start(), calls=%async_computation.1 | async-start | bytes 2359296 | tf_op jit(solution)/shard_map/all_gather | solution.py:90
  9.3 60.8 %all-gather.5.cloned.1.call-start = ((), (), s32[]{:S(2)}) async-start(), calls=%async_computation.2 | async-start | bytes 2359296 | tf_op jit(solution)/shard_map/all_gather | solution.py:91
  10.0 148.1 %reduce-scatter.2.cloned.1.call-start = ((), (), s32[]{:S(2)}) async-start(), calls=%async_computation.3 | async-start | bytes 5242880 | tf_op jit(solution)/shard_map/reduce_scatter | solution.py:104
  81.1 0.7 copy-start.2
  81.1 0.8 copy-start.1
  158.1 30.1 %copy-start = (f32[64,4096]{1,0:T(8,128)S(1)}, f32[64,4096]{1,0:T(8,128)}, u32[]{:S(2)}) copy-start(f32[64,4096]{1,0:T(8,128)} %reduce-scatter.2.cloned.1.call-done) | copy-start | bytes 3145732
  174.4 60.5 %copy-start.3 = (s32[64]{0:T(128)S(1)}, s32[64]{0:T(128)}, u32[]{:S(2)}) copy-start(s32[64]{0:T(128)} %param.13) | copy-start | bytes 772
  225.7 5.0 %collective-permute-start = (f32[8]{0:T(128)S(1)}, f32[8]{0:T(128)S(1)}, u32[]{:S(2)}, u32[]{:S(2)}) collective-permute-start(f32[8]{0:T(128)S(1)} %get-tuple-element.81), channel_id=1, source_target_pairs={{0,1},{1,2},{2,3},{4,5},{5,6},{6,7},{8,9},{9,10},{10,11},{12,13},{... | collective-permute-start | bytes 104 | tf_op jit(solution)/shard_map/ppermute | solution.py:19
  229.4 5.5 %collective-permute-start.1 = (f32[8]{0:T(128)S(1)}, f32[8]{0:T(128)S(1)}, u32[]{:S(2)}, u32[]{:S(2)}) collective-permute-start(f32[8]{0:T(128)S(1)} %get-tuple-element.82), channel_id=1, source_target_pairs={{1,0},{2,1},{3,2},{5,4},{6,5},{7,6},{9,8},{10,9},{11,10},{13,12},{... | collective-permute-start | bytes 104 | tf_op jit(solution)/shard_map/ppermute | solution.py:20
Sparse Core Ops, SparseCore 0:
  9.9 30.4 all-gather.2
  42.3 27.7 all-gather.4
  81.3 76.7 reduce-scatter.1
where the time goes:
time: 243 us; the launch traced here: 242 us
  waiting for transfers between devices  132 us (54%)
  blocking collectives  60.5 us (25%)
  matrix products  17.4 us (7%)
  between operations  13.8 us (6%)
  other arithmetic  11.4 us (5%)
  starting transfers between devices  5.05 us (2%)
    reduce_scatter x1, waiting for transfers between devices, shards(): lax.psum_scatter(jnp.concatenate([jnp.dot(all_resp, eigvecs, preferred_el...  75.6 us
    psum x4, blocking collectives, fit_block(): return lax.psum(partials, 'samp')  48.7 us
    all_gather x1, waiting for transfers between devices, shards(): lax.all_gather(weighted, 'samp', axis=0, tiled=True)  30.3 us
    all_gather x1, waiting for transfers between devices, shards(): lax.all_gather(design, 'samp', axis=0, tiled=True)  21 us
    psum x1, blocking collectives, score_block(): return lax.psum(partials, 'samp')  11.8 us
    dot_general x1, matrix products, shards(): jnp.dot(all_resp, eigvecs, preferred_element_type=jnp.float32)  8.71 us
    dot_general x1, matrix products, shards(): jnp.dot(all_design, eigvecs, preferred_element_type=jnp.float32)  8.71 us
  transfers between devices with their start and end apart: 5, of which 4 were waited for; matrix products, arithmetic and copies ran while one was open for 4% of the time, Pallas kernels for 0%

commit v1 on v0

--- a/solution.py
+++ b/solution.py
@@ -87,7 +87,15 @@
     weighted = (root_weight * responses.astype(jnp.float32)).astype(jnp.bfloat16)
     design = (root_weight * phenotype[None, :]).astype(jnp.bfloat16)
     all_resp, all_design = (
-        lax.all_gather(weighted, "samp", axis=0, tiled=True),
+        jnp.concatenate(
+            jax.lax.all_to_all(
+                jnp.stack([weighted for _ in range(jax.lax.axis_size("samp"))], 0),
+                split_axis=0,
+                axis_name="samp",
+                concat_axis=0,
+            ),
+            0,
+        ),
         lax.all_gather(design, "samp", axis=0, tiled=True),
     )
     cpg_count = lax.axis_size("cpg")

time: 243 us -> 229 us (0.942)
  waiting for transfers between devices: 132 us -> 79.4 us
  blocking collectives: 60.5 us -> 99.4 us
    all_to_all x0 -> x1, blocking collectives: none -> 38.9 us  [shards(): jax.lax.all_to_all(jnp.stack([weighted for _ in range(jax.lax.axis_size('...]
    all_gather x1 -> x0, waiting for transfers between devices: 30.3 us -> none  [shards(): lax.all_gather(weighted, 'samp', axis=0, tiled=True)]
    all_gather x1, waiting for transfers between devices: 21 us -> 0.02 us  [shards(): lax.all_gather(design, 'samp', axis=0, tiled=True)]
  transfers between devices with their start and end apart: 5 -> 4, of which waited for: 4 -> 2; matrix products, arithmetic and copies ran while one was open for 4% -> 4% of each run, Pallas kernels for 0% -> 0%
where the time goes in v1:
time: 229 us
  blocking collectives  99.4 us (43%)
  waiting for transfers between devices  79.4 us (35%)
  matrix products  16.9 us (7%)
  between operations  14.1 us (6%)
  other arithmetic  11.3 us (5%)
  starting transfers between devices  5.04 us (2%)
  local copies, waits for them, and re-layouts  2.35 us (1%)
    reduce_scatter x1, waiting for transfers between devices, shards(): lax.psum_scatter(jnp.concatenate([jnp.dot(all_resp, eigvecs, preferred_el...  75.2 us
    psum x4, blocking collectives, fit_block(): return lax.psum(partials, 'samp')  48.7 us
    all_to_all x1, blocking collectives, shards(): jax.lax.all_to_all(jnp.stack([weighted for _ in range(jax.lax.axis_size('...  38.9 us
    psum x1, blocking collectives, score_block(): return lax.psum(partials, 'samp')  11.8 us
    dot_general x1, matrix products, shards(): jnp.dot(all_design, eigvecs, preferred_element_type=jnp.float32)  8.73 us
    dot_general x1, matrix products, shards(): jnp.dot(all_resp, eigvecs, preferred_element_type=jnp.float32)  8.21 us
    reduce_sum x4, other arithmetic, fit_scores(): energy_part = jnp.sum(design_over * rot_design, axis=sum_axis)  4.81 us
  transfers between devices with their start and end apart: 4, of which 2 were waited for; matrix products, arithmetic and copies ran while one was open for 4% of the time, Pallas kernels for 0%

profile of v1, /device:TPU:0, one launch (start us, length us, event | category | flops | bytes accessed | tf_op | source)
XLA Modules:
  0.0 228.6 jit_solution(9924387359132329339)
XLA Ops:
  7.2 0.0 all-gather.2.cloned.1.call-start
  7.2 2.0 multiply_convert_fusion.1
  9.2 0.0 all-gather.2.cloned.1.call-update
  9.2 0.0 reduce-scatter.2.cloned.1.call-start
  9.2 0.2 stack.2
  9.5 38.9 %all_to_all.5 = bf16[8,32,4096]{2,1,0:T(8,128)(2,1)S(1)} all-to-all(bf16[8,32,4096]{2,1,0:T(8,128)(2,1)S(1)} %stack.2), channel_id=1, replica_groups=mesh['samp'=8,'cpg'=4] {'samp'}, dimensions={0} | all-to-all | bytes 4194304 | tf_op jit(solution)/shard_map/all_to_all | solution.py:91
  48.4 8.2 %fusion.38 = f32[256,2048]{1,0:T(8,128)S(1)} fusion(bf16[256,4096]{1,0:T(8,128)(2,1)S(1)} %bitcast.5, bf16[4096,2048]{1,0:T(8,128)(2,1)} %param.10), kind=kOutput, calls=%fused_computation.110 | convolution fusion | flops 4294967296 | bytes 20971520 | tf_op jit(solution)/shard_map/dot_general | solution.py:115
  56.6 0.0 all-gather.2.cloned.1.call-done
  56.6 8.7 %fusion.39 = f32[256,2048]{1,0:T(8,128)S(1)} fusion(bf16[256,4096]{1,0:T(8,128)(2,1)} %all-gather.2.cloned.1.call-done, bf16[4096,2048]{1,0:T(8,128)(2,1)} %param.10), kind=kOutput, calls=%fused_computation.111 | convolution fusion | flops 4294967296 | bytes 20971520 | tf_op jit(solution)/shard_map/dot_general | solution.py:116
  65.4 2.3 %pad_maximum_fusion = f32[256,4096]{1,0:T(8,128)} fusion(f32[256,2048]{1,0:T(8,128)S(1)} %fusion.39, f32[256,2048]{1,0:T(8,128)S(1)} %fusion.38), kind=kLoop, calls=%fused_computation | loop fusion | flops 1048576 | bytes 8388608 | tf_op jit(solution)/shard_map/concatenate | solution.py:113
  67.6 0.0 copy-start.2
  67.7 0.0 copy-start.1
  67.7 0.0 reduce-scatter.2.cloned.1.call-update
  67.7 0.6 copy-done.2
  68.3 0.1 pad_dynamic-slice_fusion
  68.4 0.0 copy-done.1
  68.4 0.6 multiply_multiply_fusion.14
  69.0 75.2 %reduce-scatter.2.cloned.1.call-done = f32[64,4096]{1,0:T(8,128)} async-done(((f32[256,4096]{1,0:T(8,128)}), f32[64,4096]{1,0:T(8,128)}) %reduce-scatter.2.cloned.1.call-update) | async-done | bytes 1048592 | tf_op jit(solution)/shard_map/reduce_scatter | solution.py:112
  144.3 0.0 copy-start
  144.3 1.7 fusion.7
  146.0 0.7 reduce_sum.280
  146.6 0.6 reduce_sum.282
  147.3 13.3 %all-reduce.5 = (f32[64]{0:T(128)S(1)}, f32[64]{0:T(128)S(1)}, f32[64]{0:T(128)S(1)}, f32[64]{0:T(128)S(1)}, f32[64]{0:T(128)S(1)}, /*index=5*/f32[64]{0:T(128)S(1)}, f32[64]{0:T(128)S(1)}) all-reduce(f32[64]{0:T(128)S(1)} %reduce_sum.282, f32[64]{0:T(128)S(1)} %reduce_sum.280, ...), channel_id=1, replica_groups=mesh['samp'=8,'cpg'=4] {'samp'}, use_global_device_ids=true, to_apply=%region_14.0 | all-reduce | flops 448 | bytes 3584 | tf_op jit(solution)/shard_map/psum | solution.py:107
  160.6 0.0 copy-start.3
  160.6 1.9 multiply_reduce_fusion.12
  162.5 11.8 %all-reduce.4 = (f32[64]{0:T(128)S(1)}, f32[64]{0:T(128)S(1)}, f32[64]{0:T(128)S(1)}, f32[64]{0:T(128)S(1)}, f32[64]{0:T(128)S(1)}, /*index=5*/f32[64]{0:T(128)S(1)}, f32[64]{0:T(128)S(1)}) all-reduce(f32[64]{0:T(128)S(1)} %get-tuple-element.31, f32[64]{0:T(128)S(1)} %get-tuple-element.32, ...), channel_id=1, replica_groups=mesh['samp'=8,'cpg'=4] {'samp'}, use_global_device_ids=true, to_apply=%region_28.0 | all-reduce | flops 448 | bytes 3584 | tf_op jit(solution)/shard_map/psum | solution.py:107
  174.3 0.0 copy-done
  174.3 0.6 multiply_reduce_fusion.8
  175.0 11.8 %all-reduce.3 = (f32[64]{0:T(128)S(1)}, f32[64]{0:T(128)S(1)}, f32[64]{0:T(128)S(1)}, f32[64]{0:T(128)S(1)}, f32[64]{0:T(128)S(1)}, /*index=5*/f32[64]{0:T(128)S(1)}, f32[64]{0:T(128)S(1)}) all-reduce(f32[64]{0:T(128)S(1)} %get-tuple-element.29, f32[64]{0:T(128)S(1)} %get-tuple-element.30, ...), channel_id=1, replica_groups=mesh['samp'=8,'cpg'=4] {'samp'}, use_global_device_ids=true, to_apply=%region_42.0 | all-reduce | flops 448 | bytes 3584 | tf_op jit(solution)/shard_map/psum | solution.py:107
  186.8 0.6 multiply_reduce_fusion.4
  187.4 11.8 %all-reduce.2 = (f32[64]{0:T(128)S(1)}, f32[64]{0:T(128)S(1)}, f32[64]{0:T(128)S(1)}, f32[64]{0:T(128)S(1)}, f32[64]{0:T(128)S(1)}, /*index=5*/f32[64]{0:T(128)S(1)}, f32[64]{0:T(128)S(1)}) all-reduce(f32[64]{0:T(128)S(1)} %get-tuple-element.27, f32[64]{0:T(128)S(1)} %get-tuple-element.28, ...), channel_id=1, replica_groups=mesh['samp'=8,'cpg'=4] {'samp'}, use_global_device_ids=true, to_apply=%region_56.0 | all-reduce | flops 448 | bytes 3584 | tf_op jit(solution)/shard_map/psum | solution.py:107
  199.2 0.5 fusion.32
  199.7 0.3 multiply_reduce_fusion
  200.0 11.8 %all-reduce.1 = (f32[64]{0:T(128)S(1)}, f32[64]{0:T(128)S(1)}) all-reduce(f32[64]{0:T(128)S(1)} %get-tuple-element.3, f32[64]{0:T(128)S(1)} %get-tuple-element.2), channel_id=1, replica_groups=mesh['samp'=8,'cpg'=4] {'samp'}, use_global_device_ids=true, to_apply=%region_58.0 | all-reduce | flops 128 | bytes 1024 | tf_op jit(solution)/shard_map/psum | solution.py:110
  211.8 0.1 fusion.37
  211.9 3.7 %collective-permute-start = (f32[8]{0:T(128)S(1)}, f32[8]{0:T(128)S(1)}, u32[]{:S(2)}, u32[]{:S(2)}) collective-permute-start(f32[8]{0:T(128)S(1)} %get-tuple-element.81), channel_id=1, source_target_pairs={{0,1},{1,2},{2,3},{4,5},{5,6},{6,7},{8,9},{9,10},{10,11},{12,13},{... | collective-permute-start | bytes 104 | tf_op jit(solution)/shard_map/ppermute | solution.py:19
  215.6 1.3 collective-permute-start.1
  216.9 0.0 collective-permute-done
  216.9 4.2 %collective-permute-done.1 = f32[8]{0:T(128)S(1)} collective-permute-done((f32[8]{0:T(128)S(1)}, f32[8]{0:T(128)S(1)}, u32[]{:S(2)}, u32[]{:S(2)}) %collective-permute-start.1) | collective-permute-done | bytes 64 | tf_op jit(solution)/shard_map/ppermute | solution.py:20
  221.1 0.1 pad_maximum_fusion.1
  221.1 0.0 copy-done.3
  221.1 0.6 add_divide_fusion.4
  (6 shorter events, 0.1 us)
Async XLA Ops:
  7.2 49.5 %all-gather.2.cloned.1.call-start = ((), (), s32[]{:S(2)}) async-start(), calls=%async_computation.2 | async-start | bytes 2359296 | tf_op jit(solution)/shard_map/all_gather | solution.py:99
  9.2 135.1 %reduce-scatter.2.cloned.1.call-start = ((), (), s32[]{:S(2)}) async-start(), calls=%async_computation.3 | async-start | bytes 5242880 | tf_op jit(solution)/shard_map/reduce_scatter | solution.py:112
  67.6 0.7 copy-start.2
  67.7 0.8 copy-start.1
  144.3 30.1 %copy-start = (f32[64,4096]{1,0:T(8,128)S(1)}, f32[64,4096]{1,0:T(8,128)}, u32[]{:S(2)}) copy-start(f32[64,4096]{1,0:T(8,128)} %reduce-scatter.2.cloned.1.call-done) | copy-start | bytes 3145732
  160.6 60.5 %copy-start.3 = (s32[64]{0:T(128)S(1)}, s32[64]{0:T(128)}, u32[]{:S(2)}) copy-start(s32[64]{0:T(128)} %param.13) | copy-start | bytes 772
  211.9 5.0 %collective-permute-start = (f32[8]{0:T(128)S(1)}, f32[8]{0:T(128)S(1)}, u32[]{:S(2)}, u32[]{:S(2)}) collective-permute-start(f32[8]{0:T(128)S(1)} %get-tuple-element.81), channel_id=1, source_target_pairs={{0,1},{1,2},{2,3},{4,5},{5,6},{6,7},{8,9},{9,10},{10,11},{12,13},{... | collective-permute-start | bytes 104 | tf_op jit(solution)/shard_map/ppermute | solution.py:19
  215.6 5.5 %collective-permute-start.1 = (f32[8]{0:T(128)S(1)}, f32[8]{0:T(128)S(1)}, u32[]{:S(2)}, u32[]{:S(2)}) collective-permute-start(f32[8]{0:T(128)S(1)} %get-tuple-element.82), channel_id=1, source_target_pairs={{1,0},{2,1},{3,2},{5,4},{6,5},{7,6},{9,8},{10,9},{11,10},{13,12},{... | collective-permute-start | bytes 104 | tf_op jit(solution)/shard_map/ppermute | solution.py:20
Sparse Core Ops, SparseCore 0:
  9.9 40.2 all-gather.1
  67.8 76.4 reduce-scatter.1
